TPU v7x, 32 devices: a whole 2x2x4 slice. The times are simulated.
32 devices in a mesh: dp: 16 (over z, y, x), tensor: 2 (over core).
Axes of the slice: x: 2, y: 2, z: 4, core: 2. Of those that a mesh axis runs over, the one named last changes fastest.
Arguments:
- inputs: bfloat16 [4, 8192, 768], P(None, ('dp', 'tensor')), may hold values from -6 to 6
- lengths: int32 [4, 16], P(None, 'dp'), may hold values from 128 to 512, as said below
- bounds: int32 [4, 16], P(None, 'dp'), may hold values from 32 to 384, as said below
- query_matrix: bfloat16 [768, 768], P('dp', 'tensor'), may hold values from -0.21875 to 0.21875
- key_matrix: bfloat16 [768, 768], P('dp', 'tensor'), may hold values from -0.21875 to 0.21875
- value_matrix: bfloat16 [768, 768], P('dp', 'tensor'), may hold values from -0.21875 to 0.21875
- query_value_bias: float32 [2, 768], P(None, 'tensor'), may hold values from -3 to 3
- adapter_down_weight: bfloat16 [2, 768, 8], P(None, 'dp'), may hold values from -0.21875 to 0.21875
- adapter_up_weight: bfloat16 [2, 8, 768], P(None, None, 'tensor'), may hold values from -1 to 1
- attention_output_weight: bfloat16 [768, 768], P('tensor', 'dp'), may hold values from -1.75 to 1.75
- feedforward_input_weight: bfloat16 [768, 3072], P('dp', 'tensor'), may hold values from -0.21875 to 0.21875
- feedforward_input_bias: float32 [3072], P('tensor'), may hold values from -3 to 3
- feedforward_output_weight: bfloat16 [3072, 768], P('tensor', 'dp'), may hold values from -0.109375 to 0.109375
- output_bias: float32 [2, 768], replicated, may hold values from -3 to 3
- layernorm_scale: float32 [2, 768], replicated, may hold values from 0.5 to 1.5
- layernorm_bias: float32 [2, 768], replicated, may hold values from -2 to 2
- output_gradient: bfloat16 [4, 8192, 768], P(None, ('dp', 'tensor')), may hold values from -6 to 6
Outputs:
- outputs: bfloat16 [4, 8192, 768], P(None, ('dp', 'tensor'))
- input_grad: float32 [4, 8192, 768], P(None, ('dp', 'tensor'))
- lora_up_grad: float32 [2, 8, 768], P(None, None, 'tensor')
Inputs may be any that keep to these rules, and one draw needn't show every extreme that they name: Item i of micro-batch m has live positions 0 to lengths[m, i] - 1 of its 512; the others are padding. An item's first segment is positions 0 to bounds - 1, its second bounds to 511; bounds lies between lengths // 4 and 3 * lengths // 4.
All inputs are finite; a program needn't handle non-finite values.
Results may differ from a plain program's by a relative error of at most 0.015.
The roundings to bfloat16 on the way count: a program that leaves them out, or rounds other values in their place, can miss the bound.
Values may be sent and summed in bfloat16 or wider, within the bound.
No kernel may reach another device: no remote copies, remote signals or barrier semaphores. Data moves between devices by JAX's collectives and lax.ppermute only.
A program may use at most 192 MiB of HBM per device.

v0:
```python
import jax
import jax.numpy as jnp
from jax import lax
from jax.sharding import PartitionSpec as P

HEAD_DIM = 64
UPDATE_RANK = 8
SLOT = 512
adapter_scale = 2.0
masked_value = -1000000000.0
norm_eps = 1e-05
highest_precision = lax.Precision.HIGHEST


def layer_norm(value_rows, gain, shift):
    centre = value_rows - jnp.mean(value_rows, axis=-1, keepdims=True)
    spread = jnp.mean(centre * centre, axis=-1, keepdims=True)
    return centre * lax.rsqrt(spread + norm_eps) * gain + shift


def exact_gelu(value_rows):
    return jax.nn.gelu(value_rows, approximate=False)


def item_mask(length, bound):
    places = jnp.arange(SLOT)
    segment = places >= bound
    return (places < length)[None, :] & (segment[:, None] == segment[None, :])


def split_heads(input_array):
    return input_array.reshape(input_array.shape[0], input_array.shape[1] // HEAD_DIM, HEAD_DIM)


def item_scores(query_heads, key_heads, length, bound):
    scores = (
        jnp.einsum("qhd,khd->hqk", query_heads, key_heads, preferred_element_type=jnp.float32)
        * 0.125
    )
    return jnp.where(item_mask(length, bound)[None], scores, masked_value)


def attend_forward(pieces):
    query_rows, keys, value_rows, length, bound = pieces
    query_heads = split_heads(query_rows)
    value_heads = split_heads(value_rows)
    scores = item_scores(query_heads, split_heads(keys), length, bound)
    peak = jnp.max(scores, axis=-1, keepdims=True)
    totals = jnp.log(jnp.sum(jnp.exp(scores - peak), axis=-1, keepdims=True)) + peak
    soft_weights = jnp.exp(scores - totals).astype(jnp.bfloat16)
    mixed = jnp.einsum(
        "hqk,khd->qhd", soft_weights, value_heads, preferred_element_type=jnp.float32
    )
    return (mixed.reshape(SLOT, query_rows.shape[1]).astype(jnp.bfloat16), totals)


def attend_backward(pieces):
    query_rows, keys, value_rows, grad_mixed, totals, length, bound = pieces
    query_heads = split_heads(query_rows)
    key_heads = split_heads(keys)
    grad_heads = split_heads(grad_mixed)
    scores = item_scores(query_heads, key_heads, length, bound)
    probs = jnp.exp(scores - totals)
    value_gradient = jnp.einsum(
        "hqk,qhd->khd", probs.astype(jnp.bfloat16), grad_heads, preferred_element_type=jnp.float32
    )
    grad_probs = jnp.einsum(
        "qhd,khd->hqk", grad_heads, split_heads(value_rows), preferred_element_type=jnp.float32
    )
    inner = jnp.sum(probs * grad_probs, axis=-1, keepdims=True)
    grad_scores = (probs * (grad_probs - inner)).astype(jnp.bfloat16)
    query_gradient = (
        jnp.einsum("hqk,khd->qhd", grad_scores, key_heads, preferred_element_type=jnp.float32)
        * 0.125
    )
    key_gradient = (
        jnp.einsum("hqk,qhd->khd", grad_scores, query_heads, preferred_element_type=jnp.float32)
        * 0.125
    )
    width = query_rows.shape[1]
    return (
        query_gradient.reshape(SLOT, width).astype(jnp.bfloat16),
        key_gradient.reshape(SLOT, width).astype(jnp.bfloat16),
        value_gradient.reshape(SLOT, width).astype(jnp.bfloat16),
    )


def contract_trailing(left, right):
    return lax.dot_general(
        left, right, (((1,), (1,)), ((), ())), preferred_element_type=jnp.float32
    )


def project_row_batch(
    input_rows,
    query_projected,
    key_projected,
    value_projected,
    down_projected,
    query_value_bias,
    adapter_up_weight,
):
    up_weight_float = adapter_up_weight.astype(jnp.float32)
    lowrank_update = jnp.einsum(
        "td,zdr->ztr", input_rows, down_projected, preferred_element_type=jnp.float32
    )
    query_rows = (
        jnp.dot(input_rows, query_projected, preferred_element_type=jnp.float32)
        + query_value_bias[0]
        + adapter_scale
        * jnp.dot(lowrank_update[0], up_weight_float[0], precision=highest_precision)
    ).astype(jnp.bfloat16)
    keys = jnp.dot(input_rows, key_projected, preferred_element_type=jnp.float32).astype(
        jnp.bfloat16
    )
    value_rows = (
        jnp.dot(input_rows, value_projected, preferred_element_type=jnp.float32)
        + query_value_bias[1]
        + adapter_scale
        * jnp.dot(lowrank_update[1], up_weight_float[1], precision=highest_precision)
    ).astype(jnp.bfloat16)
    return (lowrank_update, query_rows, keys, value_rows)


def adapter_components(lowrank_update, query_gradient, value_gradient):
    first_dims = (((0,), (0,)), ((), ()))
    return adapter_scale * jnp.stack(
        [
            lax.dot_general(
                lowrank_update[0],
                query_gradient.astype(jnp.float32),
                first_dims,
                precision=highest_precision,
            ),
            lax.dot_general(
                lowrank_update[1],
                value_gradient.astype(jnp.float32),
                first_dims,
                precision=highest_precision,
            ),
        ]
    )


def input_terms_all(
    query_gradient,
    key_gradient,
    value_gradient,
    query_projected,
    key_projected,
    value_projected,
    down_projected,
    adapter_up_weight,
):
    query_lowrank_gradient = adapter_scale * contract_trailing(query_gradient, adapter_up_weight[0])
    value_lowrank_gradient = adapter_scale * contract_trailing(value_gradient, adapter_up_weight[1])
    down_float = down_projected.astype(jnp.float32)
    total = contract_trailing(query_gradient, query_projected)
    total = total + contract_trailing(key_gradient, key_projected)
    total = total + contract_trailing(value_gradient, value_projected)
    total = total + lax.dot_general(
        query_lowrank_gradient, down_float[0], (((1,), (1,)), ((), ())), precision=highest_precision
    )
    total = total + lax.dot_general(
        value_lowrank_gradient, down_float[1], (((1,), (1,)), ((), ())), precision=highest_precision
    )
    return total


def forward_pass(rows_local, item_lengths, item_bounds, gathered, parameters):
    (
        query_projected,
        key_projected,
        value_projected,
        down_projected,
        out_full,
        ffn_in_full,
        ffn_out_full,
    ) = gathered
    (
        query_value_bias,
        adapter_up_weight,
        feedforward_input_bias,
        output_bias,
        layernorm_scale,
        layernorm_bias,
    ) = parameters
    group_items = item_lengths.shape[0]
    row_groups = lax.all_gather(rows_local, "tensor", axis=0, tiled=True)
    lowrank_update, query_rows, keys, value_rows = project_row_batch(
        row_groups,
        query_projected,
        key_projected,
        value_projected,
        down_projected,
        query_value_bias,
        adapter_up_weight,
    )
    width = query_rows.shape[1]
    item_shape = (group_items, SLOT, width)
    mixed, totals = lax.map(
        attend_forward,
        (
            query_rows.reshape(item_shape),
            keys.reshape(item_shape),
            value_rows.reshape(item_shape),
            item_lengths,
            item_bounds,
        ),
    )
    mixed_rows = mixed.reshape(group_items * SLOT, width)
    attended = lax.psum_scatter(
        jnp.dot(mixed_rows, out_full, preferred_element_type=jnp.float32),
        "tensor",
        scatter_dimension=0,
        tiled=True,
    )
    hidden_sum = rows_local.astype(jnp.float32) + attended + output_bias[0]
    normed = layer_norm(hidden_sum, layernorm_scale[0], layernorm_bias[0])
    pre_act = (
        jnp.dot(
            lax.all_gather(normed.astype(jnp.bfloat16), "tensor", axis=0, tiled=True),
            ffn_in_full,
            preferred_element_type=jnp.float32,
        )
        + feedforward_input_bias
    )
    activated = exact_gelu(pre_act).astype(jnp.bfloat16)
    ffn_total = (
        normed
        + lax.psum_scatter(
            jnp.dot(activated, ffn_out_full, preferred_element_type=jnp.float32),
            "tensor",
            scatter_dimension=0,
            tiled=True,
        )
        + output_bias[1]
    )
    result = layer_norm(ffn_total, layernorm_scale[1], layernorm_bias[1]).astype(jnp.bfloat16)
    kept = (lowrank_update, query_rows, keys, value_rows, totals, hidden_sum, pre_act, ffn_total)
    return (result, kept)


def layer_backward(grad_out, item_lengths, item_bounds, gathered, parameters, kept):
    (
        query_projected,
        key_projected,
        value_projected,
        down_projected,
        out_full,
        ffn_in_full,
        ffn_out_full,
    ) = gathered
    (
        query_value_bias,
        adapter_up_weight,
        feedforward_input_bias,
        output_bias,
        layernorm_scale,
        layernorm_bias,
    ) = parameters
    lowrank_update, query_rows, keys, value_rows, totals, hidden_sum, pre_act, ffn_total = kept
    group_items = item_lengths.shape[0]
    outer_pull = jax.vjp(
        lambda field: layer_norm(field, layernorm_scale[1], layernorm_bias[1]), ffn_total
    )[1]
    grad_sum = outer_pull(grad_out.astype(jnp.float32))[0]
    grad_act = contract_trailing(
        lax.all_gather(grad_sum.astype(jnp.bfloat16), "tensor", axis=0, tiled=True), ffn_out_full
    )
    gelu_pull = jax.vjp(exact_gelu, pre_act)[1]
    grad_pre = gelu_pull(grad_act)[0].astype(jnp.bfloat16)
    grad_normed = grad_sum + lax.psum_scatter(
        contract_trailing(grad_pre, ffn_in_full), "tensor", scatter_dimension=0, tiled=True
    )
    inner_pull = jax.vjp(
        lambda field: layer_norm(field, layernorm_scale[0], layernorm_bias[0]), hidden_sum
    )[1]
    grad_hidden = inner_pull(grad_normed)[0]
    grad_mixed = contract_trailing(
        lax.all_gather(grad_hidden.astype(jnp.bfloat16), "tensor", axis=0, tiled=True), out_full
    ).astype(jnp.bfloat16)
    width = query_rows.shape[1]
    item_shape = (group_items, SLOT, width)
    query_gradient, key_gradient, value_gradient = lax.map(
        attend_backward,
        (
            query_rows.reshape(item_shape),
            keys.reshape(item_shape),
            value_rows.reshape(item_shape),
            grad_mixed.reshape(item_shape),
            totals,
            item_lengths,
            item_bounds,
        ),
    )
    query_gradient = query_gradient.reshape(group_items * SLOT, width)
    key_gradient = key_gradient.reshape(group_items * SLOT, width)
    value_gradient = value_gradient.reshape(group_items * SLOT, width)
    adapter_portion = adapter_components(lowrank_update, query_gradient, value_gradient)
    row_gradient = grad_hidden + lax.psum_scatter(
        input_terms_all(
            query_gradient,
            key_gradient,
            value_gradient,
            query_projected,
            key_projected,
            value_projected,
            down_projected,
            adapter_up_weight,
        ).astype(jnp.bfloat16),
        "tensor",
        scatter_dimension=0,
        tiled=True,
    ).astype(jnp.float32)
    return (row_gradient, adapter_portion)


def local(
    inputs,
    lengths,
    bounds,
    query_matrix,
    key_matrix,
    value_matrix,
    query_value_bias,
    adapter_down_weight,
    adapter_up_weight,
    attention_output_weight,
    feedforward_input_weight,
    feedforward_input_bias,
    feedforward_output_weight,
    output_bias,
    layernorm_scale,
    layernorm_bias,
    output_gradient,
):
    micro_count = inputs.shape[0]
    parameters = (
        query_value_bias,
        adapter_up_weight,
        feedforward_input_bias,
        output_bias,
        layernorm_scale,
        layernorm_bias,
    )
    result_list = []
    gradient_tree = []
    adapter_combined = jnp.zeros((2, UPDATE_RANK, adapter_up_weight.shape[2]), jnp.float32)
    for batch_index in range(micro_count):
        forward_set = (
            lax.all_gather(query_matrix, "dp", axis=0, tiled=True),
            lax.all_gather(key_matrix, "dp", axis=0, tiled=True),
            lax.all_gather(value_matrix, "dp", axis=0, tiled=True),
            lax.all_gather(adapter_down_weight, "dp", axis=1, tiled=True),
            lax.all_gather(attention_output_weight, "dp", axis=1, tiled=True),
            lax.all_gather(feedforward_input_weight, "dp", axis=0, tiled=True),
            lax.all_gather(feedforward_output_weight, "dp", axis=1, tiled=True),
        )
        result, kept = forward_pass(
            inputs[batch_index], lengths[batch_index], bounds[batch_index], forward_set, parameters
        )
        backward_set = (
            lax.all_gather(query_matrix, "dp", axis=0, tiled=True),
            lax.all_gather(key_matrix, "dp", axis=0, tiled=True),
            lax.all_gather(value_matrix, "dp", axis=0, tiled=True),
            lax.all_gather(adapter_down_weight, "dp", axis=1, tiled=True),
            lax.all_gather(attention_output_weight, "dp", axis=1, tiled=True),
            lax.all_gather(feedforward_input_weight, "dp", axis=0, tiled=True),
            lax.all_gather(feedforward_output_weight, "dp", axis=1, tiled=True),
        )
        row_gradient, adapter_portion = layer_backward(
            output_gradient[batch_index],
            lengths[batch_index],
            bounds[batch_index],
            backward_set,
            parameters,
            kept,
        )
        adapter_combined = adapter_combined + lax.psum(adapter_portion, "dp")
        result_list.append(result)
        gradient_tree.append(row_gradient)
    return (jnp.stack(result_list), jnp.stack(gradient_tree), adapter_combined)


def solution(mesh):
    return jax.shard_map(
        local,
        mesh=mesh,
        in_specs=(
            P(None, ("dp", "tensor"), None),
            P(None, "dp"),
            P(None, "dp"),
            P("dp", "tensor"),
            P("dp", "tensor"),
            P("dp", "tensor"),
            P(None, "tensor"),
            P(None, "dp", None),
            P(None, None, "tensor"),
            P("tensor", "dp"),
            P("dp", "tensor"),
            P("tensor"),
            P("tensor", "dp"),
            P(),
            P(),
            P(),
            P(None, ("dp", "tensor"), None),
        ),
        out_specs=(
            P(None, ("dp", "tensor"), None),
            P(None, ("dp", "tensor"), None),
            P(None, None, "tensor"),
        ),
        check_vma=False,
    )
```

profile of v0, /device:TPU:0, one launch (start us, length us, event | category | flops | bytes accessed | tf_op | source)
XLA Modules:
  0.0 771.6 jit_solution(13941130316083166364)
XLA Ops:
  12.5 44.5 %all_gather.48 = bf16[2,768,8]{2,0,1:T(2,128)(2,1)S(1)} all-gather(bf16[2,48,8]{2,0,1:T(2,128)(2,1)S(1)} %copy.57), channel_id=1, replica_groups=mesh['dp'=16,'tensor'=2] {'dp'}, dimensions={1}, use_global_device_ids=true | all-gather | bytes 26112 | tf_op jit(solution)/shard_map/all_gather | solution.py:355
  57.3 39.2 %all_gather.49 = bf16[768,384]{1,0:T(8,128)(2,1)S(1)} all-gather(bf16[48,384]{1,0:T(8,128)(2,1)} %param.20), channel_id=1, replica_groups=mesh['dp'=16,'tensor'=2] {'dp'}, dimensions={0}, use_global_device_ids=true | all-gather | bytes 626688 | tf_op jit(solution)/shard_map/all_gather | solution.py:352
  96.5 41.1 %all_gather.50 = bf16[768,384]{1,0:T(8,128)(2,1)S(1)} all-gather(bf16[48,384]{1,0:T(8,128)(2,1)} %param.21), channel_id=1, replica_groups=mesh['dp'=16,'tensor'=2] {'dp'}, dimensions={0}, use_global_device_ids=true | all-gather | bytes 626688 | tf_op jit(solution)/shard_map/all_gather | solution.py:353
  137.5 39.3 %all_gather.47 = bf16[768,384]{1,0:T(8,128)(2,1)S(1)} all-gather(bf16[48,384]{1,0:T(8,128)(2,1)} %param.22), channel_id=1, replica_groups=mesh['dp'=16,'tensor'=2] {'dp'}, dimensions={0}, use_global_device_ids=true | all-gather | bytes 626688 | tf_op jit(solution)/shard_map/all_gather | solution.py:354
  176.8 40.8 %all_gather.51 = bf16[384,768]{0,1:T(8,128)(2,1)S(1)} all-gather(bf16[384,48]{0,1:T(8,128)(2,1)} %param.26), channel_id=1, replica_groups=mesh['dp'=16,'tensor'=2] {'dp'}, dimensions={1}, use_global_device_ids=true | all-gather | bytes 626688 | tf_op jit(solution)/shard_map/all_gather | solution.py:356
  218.5 2.4 all-gather.1
  232.9 3.3 all-gather
  247.4 3.1 all-gather.3
  261.4 3.2 all-gather.2
  278.0 2.6 reduce-scatter.25.cloned.1.call-done
  280.6 4.3 fusion.188
  286.7 2.8 all_gather.60
  289.5 47.2 %all-gather.7.cloned.1.call-done = bf16[768,1536]{1,0:T(8,128)(2,1)} async-done(((bf16[48,1536]{1,0:T(8,128)(2,1)}), bf16[768,1536]{1,0:T(8,128)(2,1)}) %all-gather.7.cloned.1.call-update) | async-done | bytes 2359312 | tf_op jit(solution)/shard_map/all_gather | solution.py:357
  336.7 10.4 %fusion.11 = (f32[512,1536]{1,0:T(8,128)}, f32[512,1536]{1,0:T(8,128)}) fusion(f32[1536]{0:T(1024)S(1)} %copy-done.198, bf16[512,768]{1,0:T(8,128)(2,1)S(1)} %all_gather.60, bf16[768,1536]{1,0:T(8,128)(2,1)} %all-gather.7.cloned.1.call-done), kind=kOutput, calls=%fused_computation.39 | convolution fusion | flops 1257504768 | bytes 9443328 | tf_op jit(solution)/shard_map/dot_general | solution.py:221
  347.2 52.7 %all-gather.9.cloned.1.call-done = bf16[1536,768]{0,1:T(8,128)(2,1)} async-done(((bf16[1536,48]{0,1:T(8,128)(2,1)}), bf16[1536,768]{0,1:T(8,128)(2,1)}) %all-gather.9.cloned.1.call-update) | async-done | bytes 2359312 | tf_op jit(solution)/shard_map/all_gather | solution.py:358
  399.9 6.1 fusion.35
  406.1 2.4 all_gather.58
  408.4 9.7 %fusion.10 = (f32[512,1536]{1,0:T(8,128)S(1)}, f32[512,1536]{1,0:T(8,128)S(1)}) fusion(f32[1536]{0:T(1024)} %param.28, bf16[512,768]{1,0:T(8,128)(2,1)S(1)} %all_gather.58, bf16[768,1536]{1,0:T(8,128)(2,1)} %all-gather.7.cloned.1.call-done), kind=kOutput, calls=%fused_computation.38 | convolution fusion | flops 1257504768 | bytes 9443328 | tf_op jit(solution)/shard_map/dot_general | solution.py:221
  420.8 2.7 fusion.34
  423.5 2.4 all_gather.56
  425.9 9.5 %fusion.9 = (f32[512,1536]{1,0:T(8,128)S(1)}, f32[512,1536]{1,0:T(8,128)S(1)}) fusion(f32[1536]{0:T(1024)} %param.28, bf16[512,768]{1,0:T(8,128)(2,1)S(1)} %all_gather.56, bf16[768,1536]{1,0:T(8,128)(2,1)} %all-gather.7.cloned.1.call-done), kind=kOutput, calls=%fused_computation.37 | convolution fusion | flops 1257504768 | bytes 9443328 | tf_op jit(solution)/shard_map/dot_general | solution.py:221
  438.1 2.6 fusion.33
  442.4 5.9 reduce-scatter.23.cloned.1.call-done
  448.4 4.5 fusion.187
  452.9 2.4 all_gather.52
  455.2 8.1 %fusion.8 = (f32[512,1536]{1,0:T(8,128)S(1)}, f32[512,1536]{1,0:T(8,128)S(1)}) fusion(f32[1536]{0:T(1024)S(1)} %copy-done.199, bf16[512,768]{1,0:T(8,128)(2,1)S(1)} %all_gather.52, bf16[768,1536]{1,0:T(8,128)(2,1)S(1)} %copy-done.197), kind=kOutput, calls=%fused_computation.36 | convolution fusion | flops 1257504768 | bytes 9443328 | tf_op jit(solution)/shard_map/dot_general | solution.py:221
  466.0 2.6 fusion.32
  468.7 10.4 %reduce-scatter.19.cloned.1.call-done = f32[256,768]{1,0:T(8,128)} async-done(((f32[512,768]{1,0:T(8,128)}), f32[256,768]{1,0:T(8,128)}) %reduce-scatter.19.cloned.1.call-update) | async-done | bytes 786448 | tf_op jit(solution)/shard_map/reduce_scatter | solution.py:231
  481.0 3.5 fusion.79
  486.7 2.5 all_gather.67
  489.2 7.8 %fusion.43 = f32[512,768]{1,0:T(8,128)} fusion(bf16[768,1536]{1,0:T(8,128)(2,1)} %all-gather.7.cloned.1.call-done, f32[512,1536]{1,0:T(8,128)} %get-tuple-element.339, f32[512,1536]{1,0:T(8,128)} %get-tuple-element.340, bf16[512,768]{1,0:T(8,128)(2,1)} %all_gather.67, bf16[1536,768]{0,1:T(8,128)(2,1)S(1)} %copy-done.4), kind=kOutput, calls=%fused_computation.117 | convolution fusion | flops 2426929152 | bytes 13369344 | tf_op jit(solution)/shard_map/dot_general | solution.py:89
  499.1 4.4 fusion.181
  504.5 2.5 all_gather.65
  507.1 7.8 %fusion.42 = f32[512,768]{1,0:T(8,128)} fusion(bf16[768,1536]{1,0:T(8,128)(2,1)} %all-gather.7.cloned.1.call-done, f32[512,1536]{1,0:T(8,128)} %copy-done.82, f32[512,1536]{1,0:T(8,128)} %copy-done.83, bf16[512,768]{1,0:T(8,128)(2,1)} %all_gather.65, bf16[1536,768]{0,1:T(8,128)(2,1)S(1)} %copy-done.4), kind=kOutput, calls=%fused_computation.116 | convolution fusion | flops 2426929152 | bytes 13369344 | tf_op jit(solution)/shard_map/dot_general | solution.py:89
  516.2 2.9 all_gather.61
  519.1 8.3 %fusion.40 = f32[512,768]{1,0:T(8,128)} fusion(bf16[768,1536]{1,0:T(8,128)(2,1)} %all-gather.7.cloned.1.call-done, f32[512,1536]{1,0:T(8,128)} %copy-done.84, f32[512,1536]{1,0:T(8,128)} %copy-done.85, bf16[512,768]{1,0:T(8,128)(2,1)} %all_gather.61, bf16[1536,768]{0,1:T(8,128)(2,1)S(1)} %copy-done.4), kind=kOutput, calls=%fused_computation.114 | convolution fusion | flops 2426929152 | bytes 13369344 | tf_op jit(solution)/shard_map/dot_general | solution.py:89
  528.8 2.5 all_gather.63
  531.3 7.8 %fusion.41 = f32[512,768]{1,0:T(8,128)} fusion(bf16[768,1536]{1,0:T(8,128)(2,1)} %all-gather.7.cloned.1.call-done, f32[512,1536]{1,0:T(8,128)} %copy-done.80, f32[512,1536]{1,0:T(8,128)} %copy-done.81, bf16[512,768]{1,0:T(8,128)(2,1)} %all_gather.63, bf16[1536,768]{0,1:T(8,128)(2,1)S(1)} %copy-done.4), kind=kOutput, calls=%fused_computation.115 | convolution fusion | flops 2426929152 | bytes 13369344 | tf_op jit(solution)/shard_map/dot_general | solution.py:89
  539.2 2.7 pad_maximum_fusion.1
  542.1 3.1 multiply_reduce_fusion.7
  545.2 5.8 reduce-scatter.37.cloned.1.call-done
  551.0 2.5 fusion.179
  553.7 2.5 all_gather.62
  556.9 4.6 convolution_convert_fusion.6
  564.5 2.5 all_gather.64
  572.1 2.4 all_gather.66
  580.7 2.5 all_gather.68
  588.9 4.6 multiply_reduce_fusion.3
  593.6 6.5 multiply_convert_fusion.3
  603.3 4.8 multiply_reduce_fusion.2
  608.2 4.7 multiply_reduce_fusion.1
  612.8 5.6 multiply_reduce_fusion
  622.1 6.7 multiply_convert_fusion.2
  630.5 4.9 multiply_convert_fusion.1
  637.3 4.7 multiply_convert_fusion
  647.8 2.1 add_convert_fusion.6
  650.3 2.2 convolution_bitcast_fusion.6
  657.6 2.1 add_convert_fusion.5
  659.8 2.1 convolution_bitcast_fusion.8
  667.1 2.1 add_convert_fusion.4
  676.5 77.1 %psum.34 = f32[2,8,384]{2,1,0:T(8,128)} all-reduce(f32[2,8,384]{2,1,0:T(8,128)S(1)} %fusion.110), channel_id=1, replica_groups=mesh['dp'=16,'tensor'=2] {'dp'}, use_global_device_ids=true, to_apply=%region_60.61 | all-reduce | flops 6144 | bytes 49152 | tf_op jit(solution)/shard_map/psum | solution.py:380
  755.6 2.1 add_bitcast_fusion.2
  757.7 2.1 add_bitcast_fusion.1
  761.0 3.1 pad_maximum_fusion
  (638 shorter events, 130.8 us)
Async XLA Ops:
  8.0 270.0 %reduce-scatter.21.cloned.1.call-start = ((), (), s32[]{:S(2)}) async-start(), calls=%async_computation.20 | async-start | bytes 2359296 | tf_op jit(solution)/shard_map/reduce_scatter | solution.py:212
  57.3 207.3 %copy-start.88 = (bf16[2,768,8]{1,2,0:T(8,128)(2,1)}, bf16[2,768,8]{1,2,0:T(8,128)(2,1)S(1)}, u32[]{:S(2)}) copy-start(bf16[2,768,8]{1,2,0:T(8,128)(2,1)S(1)} %copy.58) | copy-start | bytes 73732
  57.3 160.3 %copy-start.53 = (bf16[4,256,768]{2,1,0:T(8,128)(2,1)S(1)}, bf16[4,256,768]{2,1,0:T(8,128)(2,1)}, u32[]{:S(2)}) copy-start(bf16[4,256,768]{2,1,0:T(8,128)(2,1)} %param.17) | copy-start | bytes 4718596
  96.5 168.4 %copy-start.19 = (bf16[768,384]{1,0:T(8,128)(2,1)}, bf16[768,384]{1,0:T(8,128)(2,1)S(1)}, u32[]{:S(2)}) copy-start(bf16[768,384]{1,0:T(8,128)(2,1)S(1)} %all_gather.49) | copy-start | bytes 1769476
  137.5 129.9 %copy-start.14 = (bf16[768,384]{1,0:T(8,128)(2,1)}, bf16[768,384]{1,0:T(8,128)(2,1)S(1)}, u32[]{:S(2)}) copy-start(bf16[768,384]{1,0:T(8,128)(2,1)S(1)} %all_gather.50) | copy-start | bytes 1769476
  176.8 93.8 %copy-start.22 = (bf16[768,384]{1,0:T(8,128)(2,1)}, bf16[768,384]{1,0:T(8,128)(2,1)S(1)}, u32[]{:S(2)}) copy-start(bf16[768,384]{1,0:T(8,128)(2,1)S(1)} %all_gather.47) | copy-start | bytes 1769476
  217.6 56.1 %copy-start.24 = (bf16[384,768]{0,1:T(8,128)(2,1)}, bf16[384,768]{0,1:T(8,128)(2,1)S(1)}, u32[]{:S(2)}) copy-start(bf16[384,768]{0,1:T(8,128)(2,1)S(1)} %all_gather.51) | copy-start | bytes 1769476
  232.9 45.1 %reduce-scatter.17.cloned.1.call-start = ((), (), s32[]{:S(2)}) async-start(), calls=%async_computation.16 | async-start | bytes 2359296 | tf_op jit(solution)/shard_map/reduce_scatter | solution.py:212
  247.3 30.7 %reduce-scatter.29.cloned.1.call-start = ((), (), s32[]{:S(2)}) async-start(), calls=%async_computation.24 | async-start | bytes 2359296 | tf_op jit(solution)/shard_map/reduce_scatter | solution.py:212
  261.3 19.3 %reduce-scatter.25.cloned.1.call-start = ((), (), s32[]{:S(2)}) async-start(), calls=%async_computation.22 | async-start | bytes 2359296 | tf_op jit(solution)/shard_map/reduce_scatter | solution.py:212
  275.5 61.2 %all-gather.7.cloned.1.call-start = ((), (), s32[]{:S(2)}) async-start(), calls=%async_computation.17 | async-start | bytes 2506752 | tf_op jit(solution)/shard_map/all_gather | solution.py:357
  276.1 123.8 %all-gather.9.cloned.1.call-start = ((), (), s32[]{:S(2)}) async-start(), calls=%async_computation.18 | async-start | bytes 2506752 | tf_op jit(solution)/shard_map/all_gather | solution.py:358
  276.7 165.7 %reduce-scatter.31.cloned.1.call-start = ((), (), s32[]{:S(2)}) async-start(), calls=%async_computation.25 | async-start | bytes 2359296 | tf_op jit(solution)/shard_map/reduce_scatter | solution.py:231
  285.1 51.6 %copy-start.198 = (f32[1536]{0:T(1024)S(1)}, f32[1536]{0:T(1024)}, u32[]{:S(2)}) copy-start(f32[1536]{0:T(1024)} %param.28) | copy-start | bytes 18436
  406.0 36.4 %reduce-scatter.27.cloned.1.call-start = ((), (), s32[]{:S(2)}) async-start(), calls=%async_computation.23 | async-start | bytes 2359296 | tf_op jit(solution)/shard_map/reduce_scatter | solution.py:231
  408.4 12.3 %copy-start.4 = (bf16[1536,768]{0,1:T(8,128)(2,1)S(1)}, bf16[1536,768]{0,1:T(8,128)(2,1)}, u32[]{:S(2)}) copy-start(bf16[1536,768]{0,1:T(8,128)(2,1)} %all-gather.9.cloned.1.call-done) | copy-start | bytes 7077892
  423.4 24.9 %reduce-scatter.23.cloned.1.call-start = ((), (), s32[]{:S(2)}) async-start(), calls=%async_computation.21 | async-start | bytes 2359296 | tf_op jit(solution)/shard_map/reduce_scatter | solution.py:231
  438.1 10.2 %copy-start.142 = (f32[768]{0:T(1024)S(1)}, f32[768]{0:T(1024)}, u32[]{:S(2)}) copy-start(f32[768]{0:T(1024)} %get-tuple-element.175) | copy-start | bytes 9220
  438.1 10.2 %copy-start.144 = (f32[256]{0:T(256)S(1)}, f32[256]{0:T(256)}, u32[]{:S(2)}) copy-start(f32[256]{0:T(256)} %copy-done.143) | copy-start | bytes 3076
  438.1 10.2 %copy-start.148 = (f32[256]{0:T(256)S(1)}, f32[256]{0:T(256)}, u32[]{:S(2)}) copy-start(f32[256]{0:T(256)} %copy-done.147) | copy-start | bytes 3076
  438.1 10.2 %copy-start.152 = (f32[256]{0:T(256)S(1)}, f32[256]{0:T(256)}, u32[]{:S(2)}) copy-start(f32[256]{0:T(256)} %copy-done.151) | copy-start | bytes 3076
  438.1 10.2 %copy-start.165 = (f32[256]{0:T(256)S(1)}, f32[256]{0:T(256)}, u32[]{:S(2)}) copy-start(f32[256]{0:T(256)} %copy-done.164) | copy-start | bytes 3076
  438.1 10.2 %copy-start.168 = (f32[256]{0:T(256)S(1)}, f32[256]{0:T(256)}, u32[]{:S(2)}) copy-start(f32[256]{0:T(256)} %copy-done.167) | copy-start | bytes 3076
  438.1 10.2 %copy-start.171 = (f32[256]{0:T(256)S(1)}, f32[256]{0:T(256)}, u32[]{:S(2)}) copy-start(f32[256]{0:T(256)} %copy-done.170) | copy-start | bytes 3076
  440.7 38.3 %reduce-scatter.19.cloned.1.call-start = ((), (), s32[]{:S(2)}) async-start(), calls=%async_computation.19 | async-start | bytes 2359296 | tf_op jit(solution)/shard_map/reduce_scatter | solution.py:231
  442.3 10.6 %copy-start.189 = (f32[256]{0:T(256)}, f32[256]{0:T(256)S(1)}, u32[]{:S(2)}) copy-start(f32[256]{0:T(256)S(1)} %multiply_reduce_fusion.15) | copy-start | bytes 3076
  442.4 36.7 %copy-start.154 = (f32[256]{0:T(256)}, f32[256]{0:T(256)S(1)}, u32[]{:S(2)}) copy-start(f32[256]{0:T(256)S(1)} %fusion.147) | copy-start | bytes 3076
  448.4 6.9 copy-start.197
  448.4 6.9 copy-start.199
  468.6 73.4 %reduce-scatter.45.cloned.1.call-start = ((), (), s32[]{:S(2)}) async-start(), calls=%async_computation.32 | async-start | bytes 2359296 | tf_op jit(solution)/shard_map/reduce_scatter | solution.py:273
  468.6 15.8 %copy-start.179 = (f32[256]{0:T(256)}, f32[256]{0:T(256)S(1)}, u32[]{:S(2)}) copy-start(f32[256]{0:T(256)S(1)} %broadcast_multiply_fusion.4) | copy-start | bytes 3076
  468.6 15.8 %copy-start.180 = (f32[256]{0:T(256)}, f32[256]{0:T(256)S(1)}, u32[]{:S(2)}) copy-start(f32[256]{0:T(256)S(1)} %broadcast_multiply_fusion.2) | copy-start | bytes 3076
  468.7 15.8 %copy-start.182 = (f32[256]{0:T(256)}, f32[256]{0:T(256)S(1)}, u32[]{:S(2)}) copy-start(f32[256]{0:T(256)S(1)} %broadcast_multiply_fusion) | copy-start | bytes 3076
  489.2 10.0 %copy-start.141 = (f32[768]{0:T(1024)S(1)}, f32[768]{0:T(1024)}, u32[]{:S(2)}) copy-start(f32[768]{0:T(1024)} %get-tuple-element.173) | copy-start | bytes 9220
  497.0 45.0 %reduce-scatter.41.cloned.1.call-start = ((), (), s32[]{:S(2)}) async-start(), calls=%async_computation.30 | async-start | bytes 2359296 | tf_op jit(solution)/shard_map/reduce_scatter | solution.py:273
  503.5 11.4 %copy-start.158 = (f32[256]{0:T(256)}, f32[256]{0:T(256)S(1)}, u32[]{:S(2)}) copy-start(f32[256]{0:T(256)S(1)} %negate_multiply_fusion.7) | copy-start | bytes 3076
  507.1 7.9 %copy-start.196 = (f32[256]{0:T(256)S(1)}, f32[256]{0:T(256)}, u32[]{:S(2)}) copy-start(f32[256]{0:T(256)} %get-tuple-element.260) | copy-start | bytes 3076
  514.9 27.1 %reduce-scatter.33.cloned.1.call-start = ((), (), s32[]{:S(2)}) async-start(), calls=%async_computation.26 | async-start | bytes 2359296 | tf_op jit(solution)/shard_map/reduce_scatter | solution.py:273
  515.0 12.5 %copy-start.162 = (f32[256]{0:T(256)}, f32[256]{0:T(256)S(1)}, u32[]{:S(2)}) copy-start(f32[256]{0:T(256)S(1)} %negate_multiply_fusion.11) | copy-start | bytes 3076
  519.1 8.4 %copy-start.195 = (f32[256]{0:T(256)S(1)}, f32[256]{0:T(256)}, u32[]{:S(2)}) copy-start(f32[256]{0:T(256)} %get-tuple-element.194) | copy-start | bytes 3076
  527.5 23.6 %reduce-scatter.37.cloned.1.call-start = ((), (), s32[]{:S(2)}) async-start(), calls=%async_computation.28 | async-start | bytes 2359296 | tf_op jit(solution)/shard_map/reduce_scatter | solution.py:273
  539.1 214.4 %reduce-scatter.35.cloned.1.call-start = ((), (), s32[]{:S(2)}) async-start(), calls=%async_computation.27 | async-start | bytes 1179648 | tf_op jit(solution)/shard_map/reduce_scatter | solution.py:301
  541.9 9.1 %copy-start.153 = (f32[256]{0:T(256)S(1)}, f32[256]{0:T(256)}, u32[]{:S(2)}) copy-start(f32[256]{0:T(256)} %copy-done.151) | copy-start | bytes 3076
  541.9 9.1 %copy-start.155 = (f32[256]{0:T(256)S(1)}, f32[256]{0:T(256)}, u32[]{:S(2)}) copy-start(f32[256]{0:T(256)} %copy-done.154) | copy-start | bytes 3076
  541.9 9.1 %copy-start.161 = (f32[256]{0:T(256)S(1)}, f32[256]{0:T(256)}, u32[]{:S(2)}) copy-start(f32[256]{0:T(256)} %copy-done.160) | copy-start | bytes 3076
  541.9 9.1 %copy-start.163 = (f32[256]{0:T(256)S(1)}, f32[256]{0:T(256)}, u32[]{:S(2)}) copy-start(f32[256]{0:T(256)} %copy-done.162) | copy-start | bytes 3076
  556.9 10.7 %slice-start = ((s8[6291456]{0:T(1024)(128)(4,1)}), s8[4194304]{0:T(1024)(128)(4,1)S(1)}, s32[]{:S(2)}) async-start(s8[6291456]{0:T(1024)(128)(4,1)} %bitcast.410), calls=%async_computation.34 | async-start | bytes 8388608
  564.3 7.7 copy-start.34
  567.5 8.2 %slice-start.8 = ((s8[6291456]{0:T(1024)(128)(4,1)}), s8[4194304]{0:T(1024)(128)(4,1)S(1)}, s32[]{:S(2)}) async-start(s8[6291456]{0:T(1024)(128)(4,1)} %bitcast.418), calls=%async_computation.42 | async-start | bytes 8388608
  567.6 8.2 %slice-start.9 = ((s8[6291456]{0:T(1024)(128)(4,1)}), s8[2097152]{0:T(1024)(128)(4,1)S(1)}, s32[]{:S(2)}) async-start(s8[6291456]{0:T(1024)(128)(4,1)} %bitcast.418), calls=%async_computation.43 | async-start | bytes 4194304
  575.8 8.7 %slice-start.2 = ((s8[6291456]{0:T(1024)(128)(4,1)}), s8[4194304]{0:T(1024)(128)(4,1)S(1)}, s32[]{:S(2)}) async-start(s8[6291456]{0:T(1024)(128)(4,1)} %bitcast.412), calls=%async_computation.36 | async-start | bytes 8388608
  586.4 7.2 copy-start.75
  622.1 133.6 %reduce-scatter.39.cloned.1.call-start = ((), (), s32[]{:S(2)}) async-start(), calls=%async_computation.29 | async-start | bytes 1179648 | tf_op jit(solution)/shard_map/reduce_scatter | solution.py:301
  622.1 8.4 %slice-start.12 = ((s8[6291456]{0:T(1024)(128)(4,1)}), s8[4194304]{0:T(1024)(128)(4,1)S(1)}, s32[]{:S(2)}) async-start(s8[6291456]{0:T(1024)(128)(4,1)} %bitcast.422), calls=%async_computation.46 | async-start | bytes 8388608
  622.1 8.4 %slice-start.13 = ((s8[6291456]{0:T(1024)(128)(4,1)}), s8[2097152]{0:T(1024)(128)(4,1)S(1)}, s32[]{:S(2)}) async-start(s8[6291456]{0:T(1024)(128)(4,1)} %bitcast.422), calls=%async_computation.47 | async-start | bytes 4194304
  649.9 107.8 %reduce-scatter.43.cloned.1.call-start = ((), (), s32[]{:S(2)}) async-start(), calls=%async_computation.31 | async-start | bytes 1179648 | tf_op jit(solution)/shard_map/reduce_scatter | solution.py:301
  659.8 100.1 %reduce-scatter.47.cloned.1.call-start = ((), (), s32[]{:S(2)}) async-start(), calls=%async_computation.33 | async-start | bytes 1179648 | tf_op jit(solution)/shard_map/reduce_scatter | solution.py:301
  667.1 8.6 %copy-start.139 = (f32[1,8,384]{2,1,0:T(8,128)S(1)}, f32[1,8,384]{2,1,0:T(8,128)}, u32[]{:S(2)}) copy-start(f32[1,8,384]{2,1,0:T(8,128)} %convolution_bitcast_fusion.4) | copy-start | bytes 36868
  667.1 86.5 %copy-start.174 = (f32[256]{0:T(256)S(1)}, f32[256]{0:T(256)}, u32[]{:S(2)}) copy-start(f32[256]{0:T(256)} %copy-done.173) | copy-start | bytes 3076
  669.2 84.4 %copy-start.33 = (f32[256,768]{1,0:T(8,128)S(1)}, f32[256,768]{1,0:T(8,128)}, u32[]{:S(2)}) copy-start(f32[256,768]{1,0:T(8,128)} %copy-done.32) | copy-start | bytes 2359300
  669.2 86.4 %copy-start.37 = (f32[256,768]{1,0:T(8,128)S(1)}, f32[256,768]{1,0:T(8,128)}, u32[]{:S(2)}) copy-start(f32[256,768]{1,0:T(8,128)} %copy-done.36) | copy-start | bytes 2359300
  669.2 88.5 %copy-start.35 = (f32[256,768]{1,0:T(8,128)S(1)}, f32[256,768]{1,0:T(8,128)}, u32[]{:S(2)}) copy-start(f32[256,768]{1,0:T(8,128)} %copy-done.34) | copy-start | bytes 2359300
  674.2 85.6 %copy-start.40 = (f32[256,768]{1,0:T(8,128)S(1)}, f32[256,768]{1,0:T(8,128)}, u32[]{:S(2)}) copy-start(f32[256,768]{1,0:T(8,128)} %copy-done.39) | copy-start | bytes 2359300
  674.2 85.6 %copy-start.178 = (f32[256]{0:T(256)S(1)}, f32[256]{0:T(256)}, u32[]{:S(2)}) copy-start(f32[256]{0:T(256)} %copy-done.177) | copy-start | bytes 3076
  (168 other events, 570.6 us)
Sparse Core Ops, SparseCore 0:
  233.0 5.0 reduce-scatter.20
  247.4 5.1 reduce-scatter.16
  261.5 5.1 reduce-scatter.28
  275.6 4.9 reduce-scatter.24
  406.1 7.4 reduce-scatter.30
  423.6 7.4 reduce-scatter.26
  440.8 7.4 reduce-scatter.22
  468.7 10.3 reduce-scatter.18
  497.1 10.3 reduce-scatter.44
  515.0 10.3 reduce-scatter.40
  528.2 10.3 reduce-scatter.32
  540.7 10.3 reduce-scatter.36
  622.2 9.4 reduce-scatter.34
  650.1 9.4 reduce-scatter.38
  661.6 9.2 reduce-scatter.42
  673.6 9.2 reduce-scatter.46
Sparse Core Ops, SparseCore 1:
  278.8 57.9 all-gather.6
  339.4 60.4 all-gather.8
where the time goes:
time: 779 us; the launch traced here: 772 us
  blocking collectives  324 us (42%)
  matrix products  197 us (25%)
  waiting for transfers between devices  126 us (16%)
  other arithmetic  82.3 us (11%)
  local copies, waits for them, and re-layouts  22 us (3%)
  between operations  18.9 us (2%)
    psum x1, blocking collectives, local(): adapter_combined = adapter_combined + lax.psum(adapter_portion, 'dp')  77.1 us
    dot_general x28, matrix products, contract_trailing(): lax.dot_general(left, right, (((1,), (1,)), ((), ())), preferred_element_...  53.7 us
    all_gather x1, waiting for transfers between devices, local(): lax.all_gather(feedforward_output_weight, 'dp', axis=1, tiled=True)  52.7 us
    all_gather x1, waiting for transfers between devices, local(): lax.all_gather(feedforward_input_weight, 'dp', axis=0, tiled=True)  47.2 us
    all_gather x1, blocking collectives, local(): lax.all_gather(adapter_down_weight, 'dp', axis=1, tiled=True)  44.5 us
    all_gather x1, blocking collectives, local(): lax.all_gather(key_matrix, 'dp', axis=0, tiled=True)  41.1 us
    all_gather x1, blocking collectives, local(): lax.all_gather(attention_output_weight, 'dp', axis=1, tiled=True)  40.8 us
    all_gather x1, blocking collectives, local(): lax.all_gather(value_matrix, 'dp', axis=0, tiled=True)  39.3 us
  transfers between devices with their start and end apart: 18, of which 6 were waited for; matrix products, arithmetic and copies ran while one was open for 22% of the time, Pallas kernels for 0%

commit v1 on v0

--- a/solution.py
+++ b/solution.py
@@ -10,6 +10,24 @@
 masked_value = -1000000000.0
 norm_eps = 1e-05
 highest_precision = lax.Precision.HIGHEST
+
+
+def gather_around(shard, axis, dim):
+    ways, here, step = (lax.axis_size(axis), lax.axis_index(axis), shard.shape[dim])
+    dims = [n * ways if d == dim else n for d, n in enumerate(shard.shape)]
+    full = lax.dynamic_update_slice_in_dim(
+        jnp.zeros(dims, shard.dtype), shard, here * step, axis=dim
+    )
+    going_up = going_down = shard
+    for far in range(1, ways // 2 + 1):
+        going_up = lax.ppermute(going_up, axis, [(d, (d + 1) % ways) for d in range(ways)])
+        full = lax.dynamic_update_slice_in_dim(full, going_up, (here - far) % ways * step, axis=dim)
+        if 2 * far < ways:
+            going_down = lax.ppermute(going_down, axis, [(d, (d - 1) % ways) for d in range(ways)])
+            full = lax.dynamic_update_slice_in_dim(
+                full, going_down, (here + far) % ways * step, axis=dim
+            )
+    return full
 
 
 def layer_norm(value_rows, gain, shift):
@@ -353,7 +371,7 @@
             lax.all_gather(key_matrix, "dp", axis=0, tiled=True),
             lax.all_gather(value_matrix, "dp", axis=0, tiled=True),
             lax.all_gather(adapter_down_weight, "dp", axis=1, tiled=True),
-            lax.all_gather(attention_output_weight, "dp", axis=1, tiled=True),
+            gather_around(attention_output_weight, "dp", 1),
             lax.all_gather(feedforward_input_weight, "dp", axis=0, tiled=True),
             lax.all_gather(feedforward_output_weight, "dp", axis=1, tiled=True),
         )

time: 779 us -> 839 us (1.077)
  starting transfers between devices: 1.18 us -> 42.9 us
  matrix products: 197 us -> 210 us
  waiting for transfers between devices: 126 us -> 138 us
    ppermute x0 -> x15, starting transfers between devices: none -> 41.1 us  [the longest x7 36.6 us: gather_around(): lax.ppermute(going_down, axis, [(d, (d - 1) % ways) for d in range(ways)])]
    ppermute x0 -> x15, waiting for transfers between devices: none -> 17.3 us  [the longest x8 17.3 us: gather_around(): lax.ppermute(going_up, axis, [(d, (d + 1) % ways) for d in range(ways)])]
  transfers between devices with their start and end apart: 18 -> 33, of which waited for: 6 -> 12; matrix products, arithmetic and copies ran while one was open for 22% -> 24% of each run, Pallas kernels for 0% -> 0%
where the time goes in v1:
time: 839 us; the launch traced here: 835 us
  blocking collectives  318 us (38%)
  matrix products  210 us (25%)
  waiting for transfers between devices  138 us (16%)
  other arithmetic  82.8 us (10%)
  starting transfers between devices  42.9 us (5%)
  local copies, waits for them, and re-layouts  23.1 us (3%)
  between operations  19.4 us (2%)
    psum x1, blocking collectives, local(): adapter_combined = adapter_combined + lax.psum(adapter_portion, 'dp')  71.8 us
    dot_general x28, matrix products, contract_trailing(): lax.dot_general(left, right, (((1,), (1,)), ((), ())), preferred_element_...  53.6 us
    all_gather x1, waiting for transfers between devices, local(): lax.all_gather(feedforward_output_weight, 'dp', axis=1, tiled=True)  52.7 us
    all_gather x1, blocking collectives, local(): lax.all_gather(attention_output_weight, 'dp', axis=1, tiled=True)  46.8 us
    all_gather x1, waiting for transfers between devices, local(): lax.all_gather(feedforward_input_weight, 'dp', axis=0, tiled=True)  45.4 us
    all_gather x1, blocking collectives, local(): lax.all_gather(query_matrix, 'dp', axis=0, tiled=True)  40.7 us
    all_gather x1, blocking collectives, local(): lax.all_gather(adapter_down_weight, 'dp', axis=1, tiled=True)  39.7 us
    all_gather x1, blocking collectives, local(): lax.all_gather(key_matrix, 'dp', axis=0, tiled=True)  39.4 us
  transfers between devices with their start and end apart: 33, of which 12 were waited for; matrix products, arithmetic and copies ran while one was open for 24% of the time, Pallas kernels for 0%

profile of v1, /device:TPU:0, one launch (start us, length us, event | category | flops | bytes accessed | tf_op | source)
XLA Modules:
  0.0 834.6 jit_solution(10733430360642614149)
XLA Ops:
  8.0 3.0 collective-permute-start
  11.1 4.1 collective-permute-start.1
  15.9 39.7 %all_gather.48 = bf16[2,768,8]{2,0,1:T(2,128)(2,1)S(1)} all-gather(bf16[2,48,8]{2,0,1:T(2,128)(2,1)S(1)} %copy.57), channel_id=1, replica_groups=mesh['dp'=16,'tensor'=2] {'dp'}, dimensions={1}, use_global_device_ids=true | all-gather | bytes 26112 | tf_op jit(solution)/shard_map/all_gather | solution.py:373
  55.9 39.4 %all_gather.50 = bf16[768,384]{1,0:T(8,128)(2,1)S(1)} all-gather(bf16[48,384]{1,0:T(8,128)(2,1)} %param.21), channel_id=1, replica_groups=mesh['dp'=16,'tensor'=2] {'dp'}, dimensions={0}, use_global_device_ids=true | all-gather | bytes 626688 | tf_op jit(solution)/shard_map/all_gather | solution.py:371
  95.3 2.6 fusion.199
  101.1 2.4 all-gather
  104.4 40.7 %all_gather.49 = bf16[768,384]{1,0:T(8,128)(2,1)S(1)} all-gather(bf16[48,384]{1,0:T(8,128)(2,1)S(1)} %copy-done.158), channel_id=1, replica_groups=mesh['dp'=16,'tensor'=2] {'dp'}, dimensions={0}, use_global_device_ids=true | all-gather | bytes 626688 | tf_op jit(solution)/shard_map/all_gather | solution.py:370
  149.3 39.4 %all_gather.47 = bf16[768,384]{1,0:T(8,128)(2,1)S(1)} all-gather(bf16[48,384]{1,0:T(8,128)(2,1)S(1)} %copy-done.159), channel_id=1, replica_groups=mesh['dp'=16,'tensor'=2] {'dp'}, dimensions={0}, use_global_device_ids=true | all-gather | bytes 626688 | tf_op jit(solution)/shard_map/all_gather | solution.py:372
  199.1 5.4 convolution_convert_fusion.12
  205.7 2.5 exponential_reduce_fusion.3
  210.3 4.1 collective-permute-start.3
  216.6 5.7 collective-permute-start.5
  224.2 5.7 collective-permute-start.7
  231.7 5.7 collective-permute-start.9
  239.3 5.7 collective-permute-start.11
  246.8 5.7 collective-permute-start.13
  254.4 7.5 collective-permute-done.14
  262.8 3.1 fusion.211
  267.2 2.8 all-gather.3
  282.2 2.7 all-gather.2
  308.9 5.1 reduce-scatter.25.cloned.1.call-done
  314.0 3.8 fusion.188
  319.6 2.5 all_gather.59
  322.1 45.4 %all-gather.7.cloned.1.call-done = bf16[768,1536]{1,0:T(8,128)(2,1)} async-done(((bf16[48,1536]{1,0:T(8,128)(2,1)}), bf16[768,1536]{1,0:T(8,128)(2,1)}) %all-gather.7.cloned.1.call-update) | async-done | bytes 2359312 | tf_op jit(solution)/shard_map/all_gather | solution.py:375
  367.6 10.4 %fusion.11 = (f32[512,1536]{1,0:T(8,128)}, f32[512,1536]{1,0:T(8,128)}) fusion(f32[1536]{0:T(1024)S(1)} %copy-done.221, bf16[512,768]{1,0:T(8,128)(2,1)S(1)} %all_gather.59, bf16[768,1536]{1,0:T(8,128)(2,1)} %all-gather.7.cloned.1.call-done), kind=kOutput, calls=%fused_computation.39 | convolution fusion | flops 1257504768 | bytes 9443328 | tf_op jit(solution)/shard_map/dot_general | solution.py:239
  378.0 52.7 %all-gather.9.cloned.1.call-done = bf16[1536,768]{0,1:T(8,128)(2,1)} async-done(((bf16[1536,48]{0,1:T(8,128)(2,1)}), bf16[1536,768]{0,1:T(8,128)(2,1)}) %all-gather.9.cloned.1.call-update) | async-done | bytes 2359312 | tf_op jit(solution)/shard_map/all_gather | solution.py:376
  430.7 6.1 fusion.35
  439.2 9.7 %fusion.10 = (f32[512,1536]{1,0:T(8,128)S(1)}, f32[512,1536]{1,0:T(8,128)S(1)}) fusion(f32[1536]{0:T(1024)} %param.28, bf16[512,768]{1,0:T(8,128)(2,1)S(1)} %all_gather.57, bf16[768,1536]{1,0:T(8,128)(2,1)} %all-gather.7.cloned.1.call-done), kind=kOutput, calls=%fused_computation.38 | convolution fusion | flops 1257504768 | bytes 9443328 | tf_op jit(solution)/shard_map/dot_general | solution.py:239
  451.6 2.7 fusion.34
  456.7 9.5 %fusion.9 = (f32[512,1536]{1,0:T(8,128)S(1)}, f32[512,1536]{1,0:T(8,128)S(1)}) fusion(f32[1536]{0:T(1024)} %param.28, bf16[512,768]{1,0:T(8,128)(2,1)S(1)} %all_gather.55, bf16[768,1536]{1,0:T(8,128)(2,1)} %all-gather.7.cloned.1.call-done), kind=kOutput, calls=%fused_computation.37 | convolution fusion | flops 1257504768 | bytes 9443328 | tf_op jit(solution)/shard_map/dot_general | solution.py:239
  469.0 2.6 fusion.33
  473.5 5.7 reduce-scatter.23.cloned.1.call-done
  479.2 4.5 fusion.187
  486.1 8.1 fusion.8
  496.8 2.6 fusion.32
  499.5 10.4 %reduce-scatter.19.cloned.1.call-done = f32[256,768]{1,0:T(8,128)} async-done(((f32[512,768]{1,0:T(8,128)}), f32[256,768]{1,0:T(8,128)}) %reduce-scatter.19.cloned.1.call-update) | async-done | bytes 786448 | tf_op jit(solution)/shard_map/reduce_scatter | solution.py:249
  511.8 3.4 fusion.79
  517.4 2.5 all_gather.67
  519.9 7.8 fusion.43
  529.9 4.3 fusion.181
  535.3 2.5 all_gather.65
  537.8 7.8 fusion.42
  546.9 2.7 all_gather.60
  549.6 8.1 fusion.40
  559.1 2.5 all_gather.63
  561.6 7.8 fusion.41
  569.5 46.8 %all_gather.62 = bf16[384,768]{0,1:T(8,128)(2,1)} all-gather(bf16[384,48]{0,1:T(8,128)(2,1)} %param.26), channel_id=1, replica_groups=mesh['dp'=16,'tensor'=2] {'dp'}, dimensions={1}, use_global_device_ids=true | all-gather | bytes 626688 | tf_op jit(solution)/shard_map/all_gather | solution.py:386
  616.4 2.6 pad_maximum_fusion.1
  619.1 3.1 multiply_reduce_fusion.7
  622.3 2.5 fusion.179
  625.0 2.5 all_gather.61
  628.1 4.6 convolution_convert_fusion.6
  635.7 2.5 all_gather.64
  651.3 2.8 all_gather.136
  658.9 4.8 multiply_reduce_fusion.3
  663.7 4.7 multiply_convert_fusion.3
  671.7 4.8 multiply_reduce_fusion.2
  676.5 4.6 multiply_reduce_fusion.1
  681.4 5.3 multiply_reduce_fusion
  690.3 7.1 multiply_convert_fusion.2
  699.2 4.9 multiply_convert_fusion.1
  705.9 4.7 multiply_convert_fusion
  745.0 71.8 %psum.34 = f32[2,8,384]{2,1,0:T(8,128)} all-reduce(f32[2,8,384]{2,1,0:T(8,128)S(1)} %fusion.110), channel_id=1, replica_groups=mesh['dp'=16,'tensor'=2] {'dp'}, use_global_device_ids=true, to_apply=%region_60.61 | all-reduce | flops 6144 | bytes 49152 | tf_op jit(solution)/shard_map/psum | solution.py:398
  824.2 3.1 pad_maximum_fusion
  (741 shorter events, 172.9 us)
Async XLA Ops:
  8.0 300.9 %reduce-scatter.21.cloned.1.call-start = ((), (), s32[]{:S(2)}) async-start(), calls=%async_computation.20 | async-start | bytes 2359296 | tf_op jit(solution)/shard_map/reduce_scatter | solution.py:230
  8.0 200.7 %collective-permute-start = (bf16[384,48]{0,1:T(8,128)(2,1)}, bf16[384,48]{0,1:T(8,128)(2,1)}, u32[]{:S(2)}, u32[]{:S(2)}) collective-permute-start(bf16[384,48]{0,1:T(8,128)(2,1)} %param.26), channel_id=1, source_target_pairs={{0,2},{2,4},{4,6},{6,8},{8,10},{10,12},{12,14},{14,16},{16,18},{18... | collective-permute-start | bytes 110600 | tf_op jit(solution)/shard_map/ppermute | solution.py:23
  11.1 199.3 %collective-permute-start.1 = (bf16[384,48]{0,1:T(8,128)(2,1)}, bf16[384,48]{0,1:T(8,128)(2,1)}, u32[]{:S(2)}, u32[]{:S(2)}) collective-permute-start(bf16[384,48]{0,1:T(8,128)(2,1)} %param.26), channel_id=1, source_target_pairs={{0,30},{2,0},{4,2},{6,4},{8,6},{10,8},{12,10},{14,12},{16,14},{18,... | collective-permute-start | bytes 110600 | tf_op jit(solution)/shard_map/ppermute | solution.py:26
  55.9 47.6 %copy-start.95 = (bf16[2,768,8]{1,2,0:T(8,128)(2,1)}, bf16[2,768,8]{1,2,0:T(8,128)(2,1)S(1)}, u32[]{:S(2)}) copy-start(bf16[2,768,8]{1,2,0:T(8,128)(2,1)S(1)} %copy.58) | copy-start | bytes 73732
  95.3 203.1 %copy-start.14 = (bf16[768,384]{1,0:T(8,128)(2,1)}, bf16[768,384]{1,0:T(8,128)(2,1)S(1)}, u32[]{:S(2)}) copy-start(bf16[768,384]{1,0:T(8,128)(2,1)S(1)} %all_gather.50) | copy-start | bytes 1769476
  100.6 89.2 %copy-start.128 = (f32[2,512,8]{1,2,0:T(8,128)}, f32[2,512,8]{1,2,0:T(8,128)S(1)}, u32[]{:S(2)}) copy-start(f32[2,512,8]{1,2,0:T(8,128)S(1)} %convolution_bitcast_fusion.2) | copy-start | bytes 98308
  101.1 90.7 %copy-start.101 = (bf16[512,384]{0,1:T(8,128)(2,1)}, bf16[512,384]{0,1:T(8,128)(2,1)S(1)}, u32[]{:S(2)}) copy-start(bf16[512,384]{0,1:T(8,128)(2,1)S(1)} %convolution_convert_fusion.13) | copy-start | bytes 1179652
  103.5 41.7 %copy-start.82 = (bf16[1,512,768]{2,1,0:T(8,128)(2,1)}, bf16[1,512,768]{2,1,0:T(8,128)(2,1)S(1)}, u32[]{:S(2)}) copy-start(bf16[1,512,768]{2,1,0:T(8,128)(2,1)S(1)} %all-gather) | copy-start | bytes 2359300
  103.8 93.5 %copy-start.129 = (f32[2,512,8]{1,2,0:T(8,128)}, f32[2,512,8]{1,2,0:T(8,128)S(1)}, u32[]{:S(2)}) copy-start(f32[2,512,8]{1,2,0:T(8,128)S(1)} %convolution_bitcast_fusion.3) | copy-start | bytes 98308
  103.8 44.2 %copy-start.208 = (s32[4,1]{0,1:T(1,128)S(1)}, s32[4,1]{0,1:T(1,128)}, u32[]{:S(2)}) copy-start(s32[4,1]{0,1:T(1,128)} %param.18) | copy-start | bytes 52
  103.8 44.8 %copy-start.209 = (s32[4,1]{0,1:T(1,128)S(1)}, s32[4,1]{0,1:T(1,128)}, u32[]{:S(2)}) copy-start(s32[4,1]{0,1:T(1,128)} %param.19) | copy-start | bytes 52
  103.8 45.5 %copy-start.159 = (bf16[48,384]{1,0:T(8,128)(2,1)S(1)}, bf16[48,384]{1,0:T(8,128)(2,1)}, u32[]{:S(2)}) copy-start(bf16[48,384]{1,0:T(8,128)(2,1)} %param.22) | copy-start | bytes 110596
  104.4 100.1 %copy-start.103 = (bf16[512,384]{0,1:T(8,128)(2,1)}, bf16[512,384]{0,1:T(8,128)(2,1)S(1)}, u32[]{:S(2)}) copy-start(bf16[512,384]{0,1:T(8,128)(2,1)S(1)} %convolution_convert_fusion.15) | copy-start | bytes 1179652
  104.4 84.8 %copy-start.217 = (f32[384]{0:T(512)}, f32[384]{0:T(512)S(1)}, u32[]{:S(2)}) copy-start(f32[384]{0:T(512)S(1)} %get-tuple-element.188) | copy-start | bytes 4612
  145.1 145.7 %copy-start.19 = (bf16[768,384]{1,0:T(8,128)(2,1)}, bf16[768,384]{1,0:T(8,128)(2,1)S(1)}, u32[]{:S(2)}) copy-start(bf16[768,384]{1,0:T(8,128)(2,1)S(1)} %all_gather.49) | copy-start | bytes 1769476
  145.2 44.1 %copy-start.118 = (bf16[2,8,384]{2,1,0:T(8,128)(2,1)S(1)}, bf16[2,8,384]{2,1,0:T(8,128)(2,1)}, u32[]{:S(2)}) copy-start(bf16[2,8,384]{2,1,0:T(8,128)(2,1)} %param.25) | copy-start | bytes 36868
  148.0 41.8 %copy-start.120 = (f32[512,384]{0,1:T(8,128)S(1)}, f32[512,384]{0,1:T(8,128)}, u32[]{:S(2)}) copy-start(f32[512,384]{0,1:T(8,128)} %convolution_add_fusion.8) | copy-start | bytes 2359300
  197.3 81.1 %copy-start.45 = (pred[512,512]{0,1:T(8,128)(4,1)}, pred[512,512]{0,1:T(8,128)(4,1)S(1)}, u32[]{:S(2)}) copy-start(pred[512,512]{0,1:T(8,128)(4,1)S(1)} %compare_and_fusion.3) | copy-start | bytes 786436
  208.8 7.8 collective-permute-start.2
  210.3 6.3 collective-permute-start.3
  216.6 7.6 collective-permute-start.4
  216.6 7.6 collective-permute-start.5
  224.2 7.6 collective-permute-start.6
  224.2 7.6 collective-permute-start.7
  231.7 7.6 collective-permute-start.8
  231.7 7.6 collective-permute-start.9
  239.3 7.6 collective-permute-start.10
  239.3 7.6 collective-permute-start.11
  246.8 7.6 collective-permute-start.12
  246.8 7.6 collective-permute-start.13
  254.4 7.6 collective-permute-start.14
  265.9 43.0 %reduce-scatter.17.cloned.1.call-start = ((), (), s32[]{:S(2)}) async-start(), calls=%async_computation.16 | async-start | bytes 2359296 | tf_op jit(solution)/shard_map/reduce_scatter | solution.py:230
  282.1 26.8 %reduce-scatter.29.cloned.1.call-start = ((), (), s32[]{:S(2)}) async-start(), calls=%async_computation.24 | async-start | bytes 2359296 | tf_op jit(solution)/shard_map/reduce_scatter | solution.py:230
  295.9 18.1 %reduce-scatter.25.cloned.1.call-start = ((), (), s32[]{:S(2)}) async-start(), calls=%async_computation.22 | async-start | bytes 2359296 | tf_op jit(solution)/shard_map/reduce_scatter | solution.py:230
  306.4 61.2 %all-gather.7.cloned.1.call-start = ((), (), s32[]{:S(2)}) async-start(), calls=%async_computation.17 | async-start | bytes 2506752 | tf_op jit(solution)/shard_map/all_gather | solution.py:375
  307.0 123.7 %all-gather.9.cloned.1.call-start = ((), (), s32[]{:S(2)}) async-start(), calls=%async_computation.18 | async-start | bytes 2506752 | tf_op jit(solution)/shard_map/all_gather | solution.py:376
  307.5 165.9 %reduce-scatter.31.cloned.1.call-start = ((), (), s32[]{:S(2)}) async-start(), calls=%async_computation.25 | async-start | bytes 2359296 | tf_op jit(solution)/shard_map/reduce_scatter | solution.py:249
  318.0 49.5 %copy-start.221 = (f32[1536]{0:T(1024)S(1)}, f32[1536]{0:T(1024)}, u32[]{:S(2)}) copy-start(f32[1536]{0:T(1024)} %param.28) | copy-start | bytes 18436
  436.8 36.7 %reduce-scatter.27.cloned.1.call-start = ((), (), s32[]{:S(2)}) async-start(), calls=%async_computation.23 | async-start | bytes 2359296 | tf_op jit(solution)/shard_map/reduce_scatter | solution.py:249
  454.3 24.9 %reduce-scatter.23.cloned.1.call-start = ((), (), s32[]{:S(2)}) async-start(), calls=%async_computation.21 | async-start | bytes 2359296 | tf_op jit(solution)/shard_map/reduce_scatter | solution.py:249
  471.6 38.3 %reduce-scatter.19.cloned.1.call-start = ((), (), s32[]{:S(2)}) async-start(), calls=%async_computation.19 | async-start | bytes 2359296 | tf_op jit(solution)/shard_map/reduce_scatter | solution.py:249
  473.4 36.5 %copy-start.171 = (f32[256]{0:T(256)}, f32[256]{0:T(256)S(1)}, u32[]{:S(2)}) copy-start(f32[256]{0:T(256)S(1)} %fusion.147) | copy-start | bytes 3076
  499.4 119.6 %reduce-scatter.45.cloned.1.call-start = ((), (), s32[]{:S(2)}) async-start(), calls=%async_computation.32 | async-start | bytes 2359296 | tf_op jit(solution)/shard_map/reduce_scatter | solution.py:291
  499.4 15.8 %copy-start.196 = (f32[256]{0:T(256)}, f32[256]{0:T(256)S(1)}, u32[]{:S(2)}) copy-start(f32[256]{0:T(256)S(1)} %broadcast_multiply_fusion.4) | copy-start | bytes 3076
  499.5 15.8 %copy-start.197 = (f32[256]{0:T(256)}, f32[256]{0:T(256)S(1)}, u32[]{:S(2)}) copy-start(f32[256]{0:T(256)S(1)} %broadcast_multiply_fusion.2) | copy-start | bytes 3076
  499.5 15.8 %copy-start.199 = (f32[256]{0:T(256)}, f32[256]{0:T(256)S(1)}, u32[]{:S(2)}) copy-start(f32[256]{0:T(256)S(1)} %broadcast_multiply_fusion) | copy-start | bytes 3076
  527.8 91.2 %reduce-scatter.41.cloned.1.call-start = ((), (), s32[]{:S(2)}) async-start(), calls=%async_computation.30 | async-start | bytes 2359296 | tf_op jit(solution)/shard_map/reduce_scatter | solution.py:291
  545.6 73.4 %reduce-scatter.33.cloned.1.call-start = ((), (), s32[]{:S(2)}) async-start(), calls=%async_computation.26 | async-start | bytes 2359296 | tf_op jit(solution)/shard_map/reduce_scatter | solution.py:291
  557.8 64.5 %reduce-scatter.37.cloned.1.call-start = ((), (), s32[]{:S(2)}) async-start(), calls=%async_computation.28 | async-start | bytes 2359296 | tf_op jit(solution)/shard_map/reduce_scatter | solution.py:291
  569.4 49.6 %copy-start.5 = (f32[256,768]{1,0:T(8,128)S(1)}, f32[256,768]{1,0:T(8,128)}, u32[]{:S(2)}) copy-start(f32[256,768]{1,0:T(8,128)} %get-tuple-element.269) | copy-start | bytes 2359300
  569.4 49.6 %copy-start.7 = (f32[256,768]{1,0:T(8,128)S(1)}, f32[256,768]{1,0:T(8,128)}, u32[]{:S(2)}) copy-start(f32[256,768]{1,0:T(8,128)} %copy-done.6) | copy-start | bytes 2359300
  569.4 49.6 %copy-start.9 = (f32[256,768]{1,0:T(8,128)S(1)}, f32[256,768]{1,0:T(8,128)}, u32[]{:S(2)}) copy-start(f32[256,768]{1,0:T(8,128)} %copy-done.8) | copy-start | bytes 2359300
  569.4 49.6 %copy-start.162 = (f32[256]{0:T(256)S(1)}, f32[256]{0:T(256)}, u32[]{:S(2)}) copy-start(f32[256]{0:T(256)} %copy-done.160) | copy-start | bytes 3076
  569.4 49.6 %copy-start.166 = (f32[256]{0:T(256)S(1)}, f32[256]{0:T(256)}, u32[]{:S(2)}) copy-start(f32[256]{0:T(256)} %copy-done.164) | copy-start | bytes 3076
  569.5 247.3 %reduce-scatter.35.cloned.1.call-start = ((), (), s32[]{:S(2)}) async-start(), calls=%async_computation.27 | async-start | bytes 1179648 | tf_op jit(solution)/shard_map/reduce_scatter | solution.py:319
  690.2 128.6 %reduce-scatter.39.cloned.1.call-start = ((), (), s32[]{:S(2)}) async-start(), calls=%async_computation.29 | async-start | bytes 1179648 | tf_op jit(solution)/shard_map/reduce_scatter | solution.py:319
  718.5 102.4 %reduce-scatter.43.cloned.1.call-start = ((), (), s32[]{:S(2)}) async-start(), calls=%async_computation.31 | async-start | bytes 1179648 | tf_op jit(solution)/shard_map/reduce_scatter | solution.py:319
  728.3 94.7 %reduce-scatter.47.cloned.1.call-start = ((), (), s32[]{:S(2)}) async-start(), calls=%async_computation.33 | async-start | bytes 1179648 | tf_op jit(solution)/shard_map/reduce_scatter | solution.py:319
  735.6 81.1 %copy-start.191 = (f32[256]{0:T(256)S(1)}, f32[256]{0:T(256)}, u32[]{:S(2)}) copy-start(f32[256]{0:T(256)} %copy-done.190) | copy-start | bytes 3076
  737.7 79.1 %copy-start.35 = (f32[256,768]{1,0:T(8,128)S(1)}, f32[256,768]{1,0:T(8,128)}, u32[]{:S(2)}) copy-start(f32[256,768]{1,0:T(8,128)} %copy-done.34) | copy-start | bytes 2359300
  737.7 81.1 %copy-start.39 = (f32[256,768]{1,0:T(8,128)S(1)}, f32[256,768]{1,0:T(8,128)}, u32[]{:S(2)}) copy-start(f32[256,768]{1,0:T(8,128)} %copy-done.38) | copy-start | bytes 2359300
  737.7 83.2 %copy-start.37 = (f32[256,768]{1,0:T(8,128)S(1)}, f32[256,768]{1,0:T(8,128)}, u32[]{:S(2)}) copy-start(f32[256,768]{1,0:T(8,128)} %copy-done.36) | copy-start | bytes 2359300
  742.7 80.3 %copy-start.42 = (f32[256,768]{1,0:T(8,128)S(1)}, f32[256,768]{1,0:T(8,128)}, u32[]{:S(2)}) copy-start(f32[256,768]{1,0:T(8,128)} %copy-done.41) | copy-start | bytes 2359300
  742.7 80.3 %copy-start.195 = (f32[256]{0:T(256)S(1)}, f32[256]{0:T(256)}, u32[]{:S(2)}) copy-start(f32[256]{0:T(256)} %copy-done.194) | copy-start | bytes 3076
  (210 other events, 925.2 us)
Sparse Core Ops, SparseCore 0:
  266.0 4.9 reduce-scatter.20
  282.2 4.9 reduce-scatter.16
  296.0 4.9 reduce-scatter.28
  306.5 7.4 reduce-scatter.24
  436.9 7.4 reduce-scatter.30
  454.4 7.4 reduce-scatter.26
  471.7 7.4 reduce-scatter.22
  499.5 10.3 reduce-scatter.18
  527.9 10.3 reduce-scatter.44
  545.7 10.3 reduce-scatter.40
  558.9 10.3 reduce-scatter.32
  571.4 10.3 reduce-scatter.36
  690.3 4.0 reduce-scatter.34
  718.6 4.0 reduce-scatter.38
  728.4 5.6 reduce-scatter.42
  737.8 8.2 reduce-scatter.46
Sparse Core Ops, SparseCore 1:
  309.7 57.8 all-gather.6
  370.2 60.4 all-gather.8
